TPU v7x, 32 devices: a whole 2x2x4 slice. The times are simulated.
32 devices in a mesh: gx: 2 (over x), gy: 4 (over y, core), gz: 4 (over z).
Axes of the slice: x: 2, y: 2, z: 4, core: 2. Of those that a mesh axis runs over, the one named last changes fastest.
Arguments:
- tokens: bfloat16 [1024, 4608], P('gx', 'gy'), may hold values from -6 to 6
- base_up_weight: bfloat16 [4608, 18432], P('gy', ('gz', 'gx')), may hold values from -0.09375 to 0.09375
- adapter_down_weight: bfloat16 [64, 16, 4608], P(None, None, 'gy'), may hold values from -0.09375 to 0.09375
- adapter_up_weight: bfloat16 [64, 16, 18432], P('gx', None, 'gz'), may hold values from -1.5 to 1.5
- block_adapter_index: int32 [8], P('gx'), may hold values from 0 to 63
- request_rows: int32 [8], P('gx'), may hold values from 1 to 128
Outputs:
- projected: bfloat16 [1024, 18432], P(('gx', 'gy'), 'gz')
Inputs may be any that keep to these rules, and one draw needn't show every extreme that they name: `request_rows`: live rows of each block.
All inputs are finite; a program needn't handle non-finite values.
Results may differ from a plain program's by a relative error of at most 0.0047.
Values may be sent and summed in bfloat16 or wider, within the bound.
A program may use at most 128 MiB of HBM per device.

v0:
```python
import functools

import jax
import jax.numpy as jnp
from jax import lax
from jax.experimental import pallas as pl
from jax.experimental.pallas import tpu as pltpu
from jax.sharding import PartitionSpec as P

F32 = jnp.float32
BF16 = jnp.bfloat16
PIECES = 1


def general_body(
    tokens,
    base_up_weight,
    adapter_down_weight,
    adapter_up_weight,
    block_adapter_index,
    request_rows,
):
    rows, shard_width = tokens.shape
    groups = lax.axis_size("gy")
    blocks = block_adapter_index.shape[0]
    block = rows // blocks
    own_blocks = blocks // groups
    own_rows = own_blocks * block
    first = lax.axis_index("gy") * own_blocks
    count, rank_values, _ = adapter_down_weight.shape
    catalog = jnp.arange(count, dtype=jnp.int32)
    selected_adapters = (block_adapter_index[:, None] == catalog[None, :]).astype(BF16)
    chosen_down = jnp.dot(
        selected_adapters,
        adapter_down_weight.reshape(count, rank_values * shard_width),
        preferred_element_type=F32,
    )
    chosen_down = chosen_down.astype(BF16).reshape(blocks, rank_values, shard_width)
    tok_blocks = tokens.reshape(blocks, block, shard_width)
    shrink_part = jnp.einsum("bmd,brd->bmr", tok_blocks, chosen_down, preferred_element_type=F32)
    shrink_own = lax.psum_scatter(shrink_part, "gy", scatter_dimension=0, tiled=True)
    shrink_low = shrink_own.astype(BF16)
    adapter_factors = lax.all_gather(adapter_up_weight, "gx", axis=0, tiled=True)
    out_width = adapter_factors.shape[2]
    own_picks = lax.dynamic_slice_in_dim(selected_adapters, first, own_blocks, 0)
    chosen_up = jnp.dot(
        own_picks,
        adapter_factors.reshape(count, rank_values * out_width),
        preferred_element_type=F32,
    )
    chosen_up = chosen_up.astype(BF16).reshape(own_blocks, rank_values, out_width)
    expand = jnp.einsum("bmr,brf->bmf", shrink_low, chosen_up, preferred_element_type=F32)
    expand = expand.reshape(own_rows, out_width)
    partial_value = jnp.dot(
        tokens,
        lax.all_gather(base_up_weight, "gx", axis=1, tiled=True),
        preferred_element_type=F32,
    )
    extra = 2.0 * expand
    total = lax.psum_scatter(partial_value, "gy", scatter_dimension=0, tiled=True) + extra
    own_live = lax.dynamic_slice_in_dim(request_rows, first, own_blocks, 0)
    live_mask = (jnp.arange(block, dtype=jnp.int32)[None, :] < own_live[:, None]).reshape(
        own_rows, 1
    )
    return jnp.where(live_mask, total, 0.0).astype(BF16)


def kernel(
    chunks,
    index_ref,
    live_ref,
    tok_hbm,
    w_hbm,
    down_hbm,
    up_hbm,
    out_ref,
    tok,
    far_tok,
    w,
    down,
    up,
    pick,
    pick_in,
    up_own,
    up_send,
    up_in,
    shrink_own,
    shrink_send,
    shrink_in,
    a_send,
    a_in,
    keep,
    b_send,
    b_in,
    c_send,
    c_in,
    local_sem,
    a_sem,
    b_sem,
    c_sem,
    x_sem,
    z_sem,
    pick_sem,
    up_sem,
    shrink_sem,
):
    gx = lax.axis_index("gx")
    gy = lax.axis_index("gy")
    gz = lax.axis_index("gz")
    core = lax.rem(gy, 2)
    yy = lax.div(gy, 2)
    y_far = 1 - yy
    zp = lax.rem(gz, 2)
    x_peer = {"gx": 1 - gx}
    core_peer = {"gy": gy + 1 - 2 * core}
    y_peer = {"gy": lax.rem(gy + 2, 4)}
    diagonal = {"gy": 3 - gy}
    z_peer = {"gz": gz + 1 - 2 * zp}
    block = out_ref.shape[0]
    cols = w.shape[1]
    wide = cols // chunks
    ranks = down.shape[1]
    held = up.shape[0]
    piece = block // PIECES

    def remote(src, dst, sems, n, device):
        return pltpu.make_async_remote_copy(
            src_ref=src,
            dst_ref=dst,
            send_sem=sems.at[0, n],
            recv_sem=sems.at[1, n],
            device_id=device,
            device_id_type=pl.DeviceIdType.MESH,
        )

    tok_load = pltpu.make_async_copy(tok_hbm, tok, local_sem.at[0])
    tok_load.start()
    w_loads = []
    for n in range(chunks):
        span = pl.ds(n * wide, wide)
        load = pltpu.make_async_copy(w_hbm.at[:, span], w.at[:, span], local_sem.at[3 + n])
        load.start()
        w_loads.append(load)
    down_load = pltpu.make_async_copy(down_hbm, down, local_sem.at[1])
    down_load.start()
    up_load = pltpu.make_async_copy(up_hbm, up, local_sem.at[2])
    up_load.start()

    barrier = pltpu.get_barrier_semaphore()
    for device in (x_peer, core_peer, y_peer, diagonal, z_peer):
        pl.semaphore_signal(
            barrier, inc=1, device_id=device, device_id_type=pl.DeviceIdType.MESH
        )

    wanted = index_ref[gy]
    rank_at = lax.broadcasted_iota(jnp.int32, (ranks, held), 0)
    slot_at = lax.broadcasted_iota(jnp.int32, (ranks, held), 1)
    for half in range(2):
        hit = slot_at + half * held == wanted * ranks + rank_at
        pick[half] = jnp.where(hit, 1.0, 0.0).astype(BF16)

    pl.semaphore_wait(barrier, 5)
    tok_load.wait()

    x_copies, z_copies = [], []
    for u, y_at in enumerate((y_far, yy)):
        for q in range(PIECES):
            at = pl.multiple_of((2 * y_at + zp) * block + q * piece, piece)
            n = u * PIECES + q
            span = pl.ds(at, piece)
            copy = remote(tok.at[span, :], far_tok.at[span, :], x_sem, n, x_peer)
            copy.start()
            x_copies.append(copy)
            z_copies.append(remote(far_tok.at[span, :], far_tok.at[span, :], z_sem, n, z_peer))
    pick_copy = remote(pick.at[1 - gx], pick_in, pick_sem, 0, x_peer)
    pick_copy.start()

    def row(c):
        return pl.ds(pl.multiple_of(c * block, block), block)

    a_copies, b_copies, c_copies = {}, {}, {}

    def multiply(tokens_ref, g, u, y_at, n):
        s = (g * 2 + u) * chunks + n
        lhs = tokens_ref[pl.ds(pl.multiple_of(y_at * 2 * block, 2 * block), 2 * block), :]
        part = jnp.dot(lhs, w[:, n * wide : (n + 1) * wide], preferred_element_type=F32)
        low, high = part[:block], part[block:]
        mine = core == 0
        a_send[s] = jnp.where(mine, high, low)
        keep[s] = jnp.where(mine, low, high)
        copy = remote(a_send.at[s], a_in.at[s], a_sem, s, core_peer)
        copy.start()
        a_copies[s] = copy

    def pair_up(g, u, n):
        s = (g * 2 + u) * chunks + n
        a_copies[s].wait_recv()
        both = keep[s] + a_in[s]
        if u == 0:
            k = g * chunks + n
            b_send[k] = both.astype(BF16)
            copy = remote(b_send.at[k], b_in.at[k], b_sem, k, y_peer)
            copy.start()
            b_copies[k] = copy
        else:
            keep[s] = both

    def relay(n):
        x_copies[n].wait_recv()
        z_copies[n].start()

    waiting = None
    for u, y_at in enumerate((y_far, yy)):
        for n in range(chunks):
            if u == 0:
                w_loads[n].wait()
            multiply(tok, 0, u, y_at, n)
            if waiting is not None:
                pair_up(*waiting)
            waiting = (0, u, n)
    pair_up(*waiting)

    relay(0)
    down_load.wait()
    shrink_copies = []
    for d, (device, at) in enumerate(
        (
            (core_peer, core_peer["gy"]),
            (y_peer, y_peer["gy"]),
            (diagonal, diagonal["gy"]),
            (None, gy),
        )
    ):
        value = lax.dot_general(
            down[index_ref[at]],
            tok[row(at), :],
            (((1,), (1,)), ((), ())),
            preferred_element_type=F32,
        )
        if device is None:
            shrink_own[...] = value
        else:
            shrink_send[d] = value
            copy = remote(shrink_send.at[d], shrink_in.at[d], shrink_sem, d, device)
            copy.start()
            shrink_copies.append(copy)
    pick_copy.wait_recv()
    up_load.wait()
    up_width = up.shape[1]
    for n in range(2 * chunks):
        span = slice(n * wide, (n + 1) * wide)
        up_own[:, span] = jnp.dot(
            pick[gx], up[:, span], preferred_element_type=F32
        ).astype(BF16)
        up_send[:, span] = jnp.dot(
            pick_in[...], up[:, span], preferred_element_type=F32
        ).astype(BF16)
    up_copy = remote(up_send, up_in, up_sem, 0, x_peer)
    up_copy.start()

    relay(1)
    for n in range(PIECES):
        z_copies[n].wait_recv()
    waiting = None
    for n in range(chunks):
        multiply(far_tok, 1, 0, y_far, n)
        if waiting is not None:
            pair_up(*waiting)
        waiting = (1, 0, n)
    pair_up(*waiting)
    for n in range(2, 2 * PIECES):
        relay(n)
    for n in range(PIECES, 2 * PIECES):
        z_copies[n].wait_recv()
    waiting = None
    for n in range(chunks):
        multiply(far_tok, 1, 1, yy, n)
        if waiting is not None:
            pair_up(*waiting)
        waiting = (1, 1, n)
    pair_up(*waiting)

    for copy in shrink_copies:
        copy.wait_recv()
    shrink = (shrink_own[...] + shrink_in[0]) + (shrink_in[1] + shrink_in[2])
    shrink_low = shrink.astype(BF16)
    up_copy.wait_recv()
    live = lax.broadcasted_iota(jnp.int32, (block, 1), 0) < live_ref[gy]

    def finish(side, n, base):
        span = pl.ds(pl.multiple_of(side * cols + n * wide, 128), wide)
        factor = up_own[:, span] + up_in[:, span]
        expand = lax.dot_general(
            shrink_low, factor, (((0,), (0,)), ((), ())), preferred_element_type=F32
        )
        out_ref[:, span] = jnp.where(live, base + 2.0 * expand, 0.0).astype(BF16)

    for n in range(chunks):
        b_copies[n].wait_recv()
        finish(gx, n, keep[chunks + n] + b_in[n].astype(F32))
    for n in range(chunks):
        k = chunks + n
        b_copies[k].wait_recv()
        c_send[n] = (keep[3 * chunks + n] + b_in[k].astype(F32)).astype(BF16)
        copy = remote(c_send.at[n], c_in.at[n], c_sem, n, x_peer)
        copy.start()
        c_copies[n] = copy
    for n in range(chunks):
        c_copies[n].wait_recv()
        finish(1 - gx, n, c_in[n].astype(F32))

    for copy in (
        x_copies
        + z_copies
        + [pick_copy, up_copy]
        + shrink_copies
        + list(a_copies.values())
        + list(b_copies.values())
        + list(c_copies.values())
    ):
        copy.wait_send()


def fused_body(
    tokens,
    base_up_weight,
    adapter_down_weight,
    adapter_up_weight,
    block_adapter_index,
    request_rows,
):
    rows, depth = tokens.shape
    cols = base_up_weight.shape[1]
    block = rows // block_adapter_index.shape[0]
    count, ranks, _ = adapter_down_weight.shape
    held_count, _, out_width = adapter_up_weight.shape
    held = held_count * ranks
    chunks = cols // max(n for n in range(128, 1153, 128) if cols % n == 0)
    wide = cols // chunks
    steps = 4 * chunks
    anywhere = pl.BlockSpec(memory_space=pl.ANY)
    smem = pl.BlockSpec(memory_space=pltpu.SMEM)

    def dma(n):
        return pltpu.SemaphoreType.DMA((2, n))

    return pl.pallas_call(
        functools.partial(kernel, chunks),
        out_shape=jax.ShapeDtypeStruct((block, out_width), BF16),
        in_specs=[smem, smem, anywhere, anywhere, anywhere, anywhere],
        out_specs=pl.BlockSpec(memory_space=pltpu.VMEM),
        scratch_shapes=[
            pltpu.VMEM((rows, depth), BF16),
            pltpu.VMEM((rows, depth), BF16),
            pltpu.VMEM((depth, cols), BF16),
            pltpu.VMEM((count, ranks, depth), BF16),
            pltpu.VMEM((held, out_width), BF16),
            pltpu.VMEM((2, ranks, held), BF16),
            pltpu.VMEM((ranks, held), BF16),
            pltpu.VMEM((ranks, out_width), BF16),
            pltpu.VMEM((ranks, out_width), BF16),
            pltpu.VMEM((ranks, out_width), BF16),
            pltpu.VMEM((ranks, block), F32),
            pltpu.VMEM((3, ranks, block), F32),
            pltpu.VMEM((3, ranks, block), F32),
            pltpu.VMEM((steps, block, wide), F32),
            pltpu.VMEM((steps, block, wide), F32),
            pltpu.VMEM((steps, block, wide), F32),
            pltpu.VMEM((2 * chunks, block, wide), BF16),
            pltpu.VMEM((2 * chunks, block, wide), BF16),
            pltpu.VMEM((chunks, block, wide), BF16),
            pltpu.VMEM((chunks, block, wide), BF16),
            pltpu.SemaphoreType.DMA((3 + chunks,)),
            dma(steps),
            dma(2 * chunks),
            dma(chunks),
            dma(2 * PIECES),
            dma(2 * PIECES),
            dma(1),
            dma(1),
            dma(3),
        ],
        compiler_params=pltpu.CompilerParams(
            collective_id=0, has_side_effects=True, vmem_limit_bytes=60 * 1024 * 1024
        ),
    )(
        block_adapter_index,
        request_rows,
        tokens,
        base_up_weight,
        adapter_down_weight,
        adapter_up_weight.reshape(held, out_width),
    )


def solution(mesh):
    in_specs = (
        P("gx", "gy"),
        P("gy", ("gz", "gx")),
        P(None, None, "gy"),
        P("gx", None, "gz"),
        P("gx"),
        P("gx"),
    )
    out_specs = P(("gx", "gy"), "gz")
    sizes = mesh.shape

    def body(*arrays):
        blocks = arrays[4].shape[0]
        paired = sizes["gx"] == 2 and sizes["gy"] == 4 and sizes["gz"] % 2 == 0
        if paired and blocks == sizes["gy"]:
            return fused_body(*arrays)
        return general_body(*arrays)

    return jax.shard_map(body, mesh=mesh, in_specs=in_specs, out_specs=out_specs, check_vma=False)
```

profile of v0, /device:TPU:0, one launch (start us, length us, event | category | flops | bytes accessed | tf_op | source)
XLA Modules:
  0.0 50.7 jit_solution(2586818606957683466)
XLA Ops:
  0.0 48.3 %shard_map.64 = bf16[128,4608]{1,0:T(8,128)(2,1)} custom-call(s32[4]{0:T(128)} %index_ref.1, s32[4]{0:T(128)} %live_ref.1, bf16[512,1152]{1,0:T(8,128)(2,1)} %tok_hbm.1, bf16[1152,2304]{1,0:T(8,128)(2,1)} %w_hbm.1, bf16[64,16,1152]{2,1,0:T(8,128)(2,1)} %down_hbm.1, bf16[512,4608]{1,0:T(8,128)(2,1)} %bitcast.1), custom_call_target="tpu_custom_call" | custom-call | tf_op jit(solution)/shard_map/pallas_call | solution.py:347
  48.3 2.4 %copy.8 = bf16[128,4608]{1,0:T(8,128)(2,1)} copy(bf16[128,4608]{1,0:T(8,128)(2,1)} %shard_map.64) | data formatting | bytes 2359296
where the time goes:
time: 50.8 us; the launch traced here: 50.7 us
  Pallas kernels  48.3 us (95%)
  local copies, waits for them, and re-layouts  2.36 us (5%)
    pallas_call x1, Pallas kernels, fused_body(): pl.pallas_call(functools.partial(kernel, chunks), out_shape=jax.ShapeDtyp...  48.3 us
    unnamed x1, local copies, waits for them, and re-layouts  2.36 us

commit v1 on v0

v1 whole, which is shorter than its diff:
```python
import functools

import jax
import jax.numpy as jnp
from jax import lax
from jax.experimental import pallas as pl
from jax.experimental.pallas import tpu as pltpu
from jax.sharding import PartitionSpec as P

F32 = jnp.float32
BF16 = jnp.bfloat16
STAGES = 4
FAR_PARTS = 3
MESH = pl.DeviceIdType.MESH


def general_body(
    tokens,
    base_up_weight,
    adapter_down_weight,
    adapter_up_weight,
    block_adapter_index,
    request_rows,
):
    rows, shard_width = tokens.shape
    groups = lax.axis_size("gy")
    blocks = block_adapter_index.shape[0]
    block = rows // blocks
    own_blocks = blocks // groups
    own_rows = own_blocks * block
    first = lax.axis_index("gy") * own_blocks
    count, rank_values, _ = adapter_down_weight.shape
    catalog = jnp.arange(count, dtype=jnp.int32)
    selected_adapters = (block_adapter_index[:, None] == catalog[None, :]).astype(BF16)
    chosen_down = jnp.dot(
        selected_adapters,
        adapter_down_weight.reshape(count, rank_values * shard_width),
        preferred_element_type=F32,
    )
    chosen_down = chosen_down.astype(BF16).reshape(blocks, rank_values, shard_width)
    tok_blocks = tokens.reshape(blocks, block, shard_width)
    shrink_part = jnp.einsum("bmd,brd->bmr", tok_blocks, chosen_down, preferred_element_type=F32)
    shrink_own = lax.psum_scatter(shrink_part, "gy", scatter_dimension=0, tiled=True)
    shrink_low = shrink_own.astype(BF16)
    adapter_factors = lax.all_gather(adapter_up_weight, "gx", axis=0, tiled=True)
    out_width = adapter_factors.shape[2]
    own_picks = lax.dynamic_slice_in_dim(selected_adapters, first, own_blocks, 0)
    chosen_up = jnp.dot(
        own_picks,
        adapter_factors.reshape(count, rank_values * out_width),
        preferred_element_type=F32,
    )
    chosen_up = chosen_up.astype(BF16).reshape(own_blocks, rank_values, out_width)
    expand = jnp.einsum("bmr,brf->bmf", shrink_low, chosen_up, preferred_element_type=F32)
    expand = expand.reshape(own_rows, out_width)
    partial_value = jnp.dot(
        tokens,
        lax.all_gather(base_up_weight, "gx", axis=1, tiled=True),
        preferred_element_type=F32,
    )
    extra = 2.0 * expand
    total = lax.psum_scatter(partial_value, "gy", scatter_dimension=0, tiled=True) + extra
    own_live = lax.dynamic_slice_in_dim(request_rows, first, own_blocks, 0)
    live_mask = (jnp.arange(block, dtype=jnp.int32)[None, :] < own_live[:, None]).reshape(
        own_rows, 1
    )
    return jnp.where(live_mask, total, 0.0).astype(BF16)


def kernel(
    near_spans,
    far_spans,
    index_hbm,
    live_hbm,
    tok_hbm,
    w_hbm,
    down_hbm,
    up_hbm,
    out_ref,
    index_ref,
    live_ref,
    tok,
    far_tok,
    w,
    down,
    up,
    name_send,
    name_in,
    up_own,
    up_send,
    up_in,
    up_peer,
    shrink_own,
    shrink_send,
    shrink_in,
    low_send,
    low_in,
    far_extra,
    peer_extra,
    a_send,
    a_in,
    keep,
    fa_send,
    fa_in,
    fkeep,
    b_send,
    b_in,
    fb_send,
    fb_in,
    c_send,
    c_in,
    load_sem,
    w_sem,
    a_sem,
    fa_sem,
    b_sem,
    fb_sem,
    c_sem,
    x_sem,
    z_sem,
    shrink_sem,
    name_sem,
    low_sem,
    up_sem,
):
    gx = lax.axis_index("gx")
    gy = lax.axis_index("gy")
    gz = lax.axis_index("gz")
    core = lax.rem(gy, 2)
    yy = lax.div(gy, 2)
    y_far = 1 - yy
    zp = lax.rem(gz, 2)
    x_peer = {"gx": 1 - gx}
    core_peer = {"gy": gy + 1 - 2 * core}
    y_peer = {"gy": lax.rem(gy + 2, 4)}
    diagonal = {"gy": 3 - gy}
    z_peer = {"gz": gz + 1 - 2 * zp}
    block = out_ref.shape[0]
    cols = w.shape[1]
    held, ranks, _ = up.shape
    part_rows = block // STAGES
    near = len(near_spans)
    far = len(far_spans)

    def remote(src, dst, sems, n, device):
        return pltpu.make_async_remote_copy(
            src_ref=src,
            dst_ref=dst,
            send_sem=sems.at[0],
            recv_sem=sems.at[1 + n],
            device_id=device,
            device_id_type=MESH,
        )

    def rows_at(block_at, first, count):
        return pl.ds(pl.multiple_of(block_at * block + first, count), count)

    def load(src, dst, sem):
        copy = pltpu.make_async_copy(src, dst, sem)
        copy.start()
        return copy

    def tok_half(y_at, n):
        span = pl.ds(pl.multiple_of(y_at * 2 * block, 2 * block), 2 * block)
        return load(tok_hbm.at[span, :], tok.at[span, :], load_sem.at[n])

    def w_load(n):
        start, width = near_spans[n]
        span = pl.ds(start, width)
        return load(w_hbm.at[:, span], w.at[:, span], w_sem.at[n])

    tok_far_load = tok_half(y_far, 0)
    w_loads = [w_load(0)]
    tok_own_load = tok_half(yy, 1)
    index_load = load(index_hbm, index_ref, load_sem.at[2])
    live_load = load(live_hbm, live_ref, load_sem.at[3])
    w_loads += [w_load(n) for n in range(1, 3)]
    down_load = load(down_hbm, down, load_sem.at[4])
    w_loads += [w_load(n) for n in range(3, near)]
    up_load = load(up_hbm, up, load_sem.at[5])

    barrier = pltpu.get_barrier_semaphore()
    for device in (x_peer, core_peer, y_peer, diagonal, z_peer):
        pl.semaphore_signal(barrier, inc=1, device_id=device, device_id_type=MESH)

    def go(copy):
        copy.start()
        return copy

    x_copies, z_copies = [], []
    for r in range(STAGES):
        for y_at in (y_far, yy):
            n = len(x_copies)
            span = rows_at(2 * y_at + zp, r * part_rows, part_rows)
            x_copies.append(remote(tok.at[span, :], far_tok.at[span, :], x_sem, n, x_peer))
            z_copies.append(
                remote(far_tok.at[span, :], far_tok.at[span, :], z_sem, n, z_peer)
            )

    def relay(n):
        x_copies[n].wait_recv()
        go(z_copies[n])

    a_copies, fa_copies, b_copies, fb_copies, c_copies = {}, {}, {}, {}, {}

    def near_dot(u, n):
        y_at = (y_far, yy)[u]
        start, width = near_spans[n]
        lhs = jnp.concatenate(
            [
                tok[rows_at(2 * y_at + 1 - core, 0, block), :],
                tok[rows_at(2 * y_at + core, 0, block), :],
            ],
            axis=0,
        )
        span = slice(start, start + width)
        part = jnp.dot(lhs, w[:, span], preferred_element_type=F32)
        a_send[u, :, span] = part[:block]
        keep[u, :, span] = part[block:]

    def near_give(u, n):
        start, width = near_spans[n]
        span = pl.ds(start, width)
        a_copies[u, n] = go(
            remote(
                a_send.at[u, :, span], a_in.at[u, :, span], a_sem, u * near + n, core_peer
            )
        )

    def near_pair(n, hold=False):
        start, width = near_spans[n]
        span = pl.ds(start, width)
        a_copies[0, n].wait_recv()
        b_send[:, span] = (keep[0, :, span] + a_in[0, :, span]).astype(BF16)
        b_copies[n] = remote(b_send.at[:, span], b_in.at[:, span], b_sem, n, y_peer)
        if not hold:
            go(b_copies[n])

    def far_dot(h, n):
        start, width = far_spans[n]
        lhs = jnp.concatenate(
            [
                far_tok[rows_at(2 * y_at + c, h * part_rows, part_rows), :]
                for c in (1 - core, core)
                for y_at in (y_far, yy)
            ],
            axis=0,
        )
        span = slice(start, start + width)
        part = jnp.dot(lhs, w[:, span], preferred_element_type=F32)
        fa_send[h, :, span] = part[: 2 * part_rows]
        fkeep[h, :, span] = part[2 * part_rows :]
        span = pl.ds(start, width)
        fa_copies[h, n] = go(
            remote(
                fa_send.at[h, :, span], fa_in.at[h, :, span], fa_sem, h * far + n, core_peer
            )
        )

    def far_pair(h, n):
        start, width = far_spans[n]
        span = pl.ds(start, width)
        fa_copies[h, n].wait_recv()
        out_rows = pl.ds(0, part_rows)
        fb_send[h, :, span] = (fkeep[h, out_rows, span] + fa_in[h, out_rows, span]).astype(
            BF16
        )
        fb_copies[h, n] = go(
            remote(fb_send.at[h, :, span], fb_in.at[h, :, span], fb_sem, h * far + n, y_peer)
        )

    def far_return(h, n):
        start, width = far_spans[n]
        span = pl.ds(start, width)
        own_rows = pl.ds(part_rows, part_rows)
        fb_copies[h, n].wait_recv()
        total = fkeep[h, own_rows, span] + fa_in[h, own_rows, span]
        total += fb_in[h, :, span].astype(F32)
        total += peer_extra[pl.ds(h * part_rows, part_rows), span]
        c_send[h, :, span] = total.astype(BF16)
        c_copies[h, n] = go(
            remote(c_send.at[h, :, span], c_in.at[h, :, span], c_sem, h * far + n, x_peer)
        )

    def expanded(low, factor):
        return 2.0 * lax.dot_general(
            low, factor, (((0,), (0,)), ((), ())), preferred_element_type=F32
        )

    def live_rows(first, count):
        at = lax.broadcasted_iota(jnp.int32, (count, 1), 0) + first
        return at < live_ref[gy]

    def out_span(side, start, width):
        return pl.ds(pl.multiple_of(side * cols + start, 128), width)

    def finish_near(n):
        start, width = near_spans[n]
        span = pl.ds(start, width)
        a_copies[1, n].wait_recv()
        b_copies[n].wait_recv()
        total = keep[1, :, span] + a_in[1, :, span] + b_in[:, span].astype(F32)
        factor = up_own[:, out_span(gx, start, width)] + up_in[:, span]
        total += expanded(low_send[...], factor)
        out_ref[:, out_span(gx, start, width)] = jnp.where(
            live_rows(0, block), total, 0.0
        ).astype(BF16)

    def finish_far(h, n):
        start, width = far_spans[n]
        span = pl.ds(start, width)
        c_copies[h, n].wait_recv()
        rows = pl.ds(h * part_rows, part_rows)
        total = c_in[h, :, span].astype(F32) + far_extra[rows, span]
        out_ref[rows, out_span(1 - gx, start, width)] = jnp.where(
            live_rows(h * part_rows, part_rows), total, 0.0
        ).astype(BF16)

    def near_step(u, n):
        if u == 0:
            w_loads[n].wait()
        near_dot(u, n)
        near_give(u, n)

    tok_far_load.wait()
    w_loads[0].wait()
    near_dot(0, 0)
    tok_own_load.wait()
    index_load.wait()
    live_load.wait()
    name_send[...] = jnp.full(name_send.shape, index_ref[gy].astype(F32))
    pl.semaphore_wait(barrier, 5)
    near_give(0, 0)
    name_copy = go(remote(name_send, name_in, name_sem, 0, x_peer))
    early = len(x_copies) - 2
    for n in range(early):
        go(x_copies[n])

    shrink_copies = []

    def shrink_part(at):
        return lax.dot_general(
            down[index_ref[at]],
            tok[rows_at(at, 0, block), :],
            (((1,), (1,)), ((), ())),
            preferred_element_type=F32,
        )

    def shrink_give(d, device):
        shrink_send[d] = shrink_part(device["gy"])
        shrink_copies.append(
            go(remote(shrink_send.at[d], shrink_in.at[d], shrink_sem, d, device))
        )

    near_step(0, 1)
    near_step(0, 2)
    near_pair(0)
    down_load.wait()
    shrink_give(0, y_peer)
    shrink_give(1, diagonal)
    near_pair(1)
    near_step(0, 3)
    shrink_give(2, core_peer)
    near_pair(2)
    for n in range(4, near):
        near_step(0, n)
    shrink_own[...] = shrink_part(gy)
    for n in range(3, near - 1):
        near_pair(n)
    relay(0)
    near_pair(near - 1, hold=True)

    up_load.wait()
    slot = index_ref[gy] - gx * held
    mine = up[jnp.clip(slot, 0, held - 1)]
    here = jnp.logical_and(slot >= 0, slot < held)
    up_own[...] = jnp.where(here, mine, jnp.zeros_like(mine))
    name_copy.wait_recv()
    rank_at = lax.broadcasted_iota(jnp.int32, (ranks, held * ranks), 0)
    slot_at = lax.broadcasted_iota(jnp.int32, (ranks, held * ranks), 1) + gx * held * ranks
    wanted = name_in[0:1, 0:1] * float(ranks)
    hit = (slot_at - rank_at).astype(F32) == wanted
    pick = jnp.where(hit, 1.0, 0.0).astype(BF16)

    def picked(side, start, width):
        factors = up[:, :, out_span(side, start, width)].reshape(held * ranks, width)
        return jnp.dot(pick, factors, preferred_element_type=F32).astype(BF16)

    for start, width in far_spans:
        up_send[:, pl.ds(start, width)] = picked(1 - gx, start, width)
    for copy in shrink_copies:
        copy.wait_recv()
    shrink = (shrink_own[...] + shrink_in[0]) + (shrink_in[1] + shrink_in[2])
    low_send[...] = shrink.astype(BF16)
    low_copy = go(remote(low_send, low_in, low_sem, 0, x_peer))
    for n in range(early, len(x_copies)):
        go(x_copies[n])
    up_copy = go(remote(up_send, up_in, up_sem, 0, x_peer))
    near_step(1, 0)
    near_step(1, 1)
    relay(1)
    for start, width in far_spans:
        up_peer[:, pl.ds(start, width)] = picked(gx, start, width)
    near_step(1, 2)
    relay(2)
    for n in range(3, near):
        near_step(1, n)

    relay(3)

    def far_tokens(h):
        z_copies[2 * h].wait_recv()
        z_copies[2 * h + 1].wait_recv()

    far_tokens(0)
    for n in range(far):
        far_dot(0, n)
    relay(4)
    for start, width in far_spans:
        far_extra[:, pl.ds(start, width)] = expanded(
            low_send[...], up_own[:, out_span(1 - gx, start, width)]
        )
    for n in range(far):
        far_pair(0, n)
    relay(5)
    far_tokens(1)
    for n in range(far):
        far_dot(1, n)
    relay(6)
    low_copy.wait_recv()
    for start, width in far_spans:
        span = pl.ds(start, width)
        peer_extra[:, span] = expanded(low_in[...], up_peer[:, span])
    for n in range(far):
        far_pair(1, n)
    relay(7)
    far_tokens(2)
    far_dot(2, 0)
    far_return(0, 0)
    far_dot(2, 1)
    far_dot(2, 2)
    far_return(0, 1)
    far_pair(2, 0)
    far_pair(2, 1)
    far_return(0, 2)
    far_pair(2, 2)
    far_tokens(3)
    far_dot(3, 0)
    far_return(1, 0)
    far_dot(3, 1)
    far_dot(3, 2)
    far_return(1, 1)
    for n in range(far):
        far_pair(3, n)
    go(b_copies[near - 1])
    far_return(1, 2)
    up_copy.wait_recv()
    for n in range(0, near - 1):
        finish_near(n)
    for n in range(far):
        far_return(2, n)
    for n in range(far):
        finish_far(0, n)
    for n in range(far):
        finish_far(1, n)
    for n in range(far):
        far_return(3, n)
    for n in range(far):
        finish_far(2, n)
    finish_near(near - 1)
    for n in range(far):
        finish_far(3, n)

    half = pl.ds(0, 2 * block)
    for src, sems in (
        (a_send, a_sem),
        (fa_send, fa_sem),
        (b_send, b_sem),
        (fb_send, fb_sem),
        (c_send, c_sem),
        (tok.at[half, :], x_sem),
        (tok.at[half, :], z_sem),
        (shrink_send, shrink_sem),
        (name_send, name_sem),
        (low_send, low_sem),
        (up_send, up_sem),
    ):
        remote(src, src, sems, 0, x_peer).wait_send()


def spans_of(cols, first, wide):
    spans, start = [], 0
    while start < cols:
        width = min(wide if start else first, cols - start)
        spans.append((start, width))
        start += width
    return spans


def fused_body(
    tokens,
    base_up_weight,
    adapter_down_weight,
    adapter_up_weight,
    block_adapter_index,
    request_rows,
):
    rows, depth = tokens.shape
    cols = base_up_weight.shape[1]
    blocks = block_adapter_index.shape[0]
    block = rows // blocks
    count, ranks, _ = adapter_down_weight.shape
    held, _, out_width = adapter_up_weight.shape
    near_spans = spans_of(cols, 256, 512)
    far_spans = spans_of(cols, cols // FAR_PARTS, cols // FAR_PARTS)
    near, far = len(near_spans), len(far_spans)
    part_rows = block // STAGES
    in_hbm = pl.BlockSpec(memory_space=pltpu.HBM)

    def dma(n):
        return pltpu.SemaphoreType.DMA((1 + n,))

    return pl.pallas_call(
        functools.partial(kernel, near_spans, far_spans),
        out_shape=pltpu.VMEM((block, out_width), BF16),
        in_specs=[in_hbm] * 6,
        out_specs=pl.BlockSpec(memory_space=pltpu.VMEM),
        scratch_shapes=[
            pltpu.SMEM((blocks,), jnp.int32),
            pltpu.SMEM((blocks,), jnp.int32),
            pltpu.VMEM((rows, depth), BF16),
            pltpu.VMEM((rows, depth), BF16),
            pltpu.VMEM((depth, cols), BF16),
            pltpu.VMEM((count, ranks, depth), BF16),
            pltpu.VMEM((held, ranks, out_width), BF16),
            pltpu.VMEM((8, 128), F32),
            pltpu.VMEM((8, 128), F32),
            pltpu.VMEM((ranks, out_width), BF16),
            pltpu.VMEM((ranks, cols), BF16),
            pltpu.VMEM((ranks, cols), BF16),
            pltpu.VMEM((ranks, cols), BF16),
            pltpu.VMEM((ranks, block), F32),
            pltpu.VMEM((3, ranks, block), F32),
            pltpu.VMEM((3, ranks, block), F32),
            pltpu.VMEM((ranks, block), BF16),
            pltpu.VMEM((ranks, block), BF16),
            pltpu.VMEM((block, cols), F32),
            pltpu.VMEM((block, cols), F32),
            pltpu.VMEM((2, block, cols), F32),
            pltpu.VMEM((2, block, cols), F32),
            pltpu.VMEM((2, block, cols), F32),
            pltpu.VMEM((STAGES, 2 * part_rows, cols), F32),
            pltpu.VMEM((STAGES, 2 * part_rows, cols), F32),
            pltpu.VMEM((STAGES, 2 * part_rows, cols), F32),
            pltpu.VMEM((block, cols), BF16),
            pltpu.VMEM((block, cols), BF16),
            pltpu.VMEM((STAGES, part_rows, cols), BF16),
            pltpu.VMEM((STAGES, part_rows, cols), BF16),
            pltpu.VMEM((STAGES, part_rows, cols), BF16),
            pltpu.VMEM((STAGES, part_rows, cols), BF16),
            pltpu.SemaphoreType.DMA((6,)),
            pltpu.SemaphoreType.DMA((near,)),
            dma(2 * near),
            dma(STAGES * far),
            dma(near),
            dma(STAGES * far),
            dma(STAGES * far),
            dma(2 * STAGES),
            dma(2 * STAGES),
            dma(3),
            dma(1),
            dma(1),
            dma(1),
        ],
        compiler_params=pltpu.CompilerParams(
            collective_id=0, has_side_effects=True, vmem_limit_bytes=56 * 1024 * 1024
        ),
    )(
        block_adapter_index,
        request_rows,
        tokens,
        base_up_weight,
        adapter_down_weight,
        adapter_up_weight,
    )


def solution(mesh):
    in_specs = (
        P("gx", "gy"),
        P("gy", ("gz", "gx")),
        P(None, None, "gy"),
        P("gx", None, "gz"),
        P("gx"),
        P("gx"),
    )
    out_specs = P(("gx", "gy"), "gz")
    sizes = mesh.shape

    def body(*arrays):
        blocks = arrays[4].shape[0]
        paired = sizes["gx"] == 2 and sizes["gy"] == 4 and sizes["gz"] % 2 == 0
        cols = arrays[1].shape[1]
        cut = cols % (FAR_PARTS * 128) == 0 and len(spans_of(cols, 256, 512)) > 4
        cut = cut and arrays[0].shape[0] // blocks % (STAGES * 16) == 0
        if paired and cut and blocks == sizes["gy"]:
            return fused_body(*arrays)
        return general_body(*arrays)

    return jax.shard_map(body, mesh=mesh, in_specs=in_specs, out_specs=out_specs, check_vma=False)
```

time: 50.8 us -> 38.5 us (0.76)
  Pallas kernels: 48.3 us -> 37.3 us
  local copies, waits for them, and re-layouts: 2.36 us -> 1.02 us
    pallas_call x1, Pallas kernels: 48.3 us -> 37.3 us  [fused_body(): pl.pallas_call(functools.partial(kernel, near_spans, far_spans), out_shap...]
    unnamed x1, local copies, waits for them, and re-layouts: 2.36 us -> 1.02 us
where the time goes in v1:
time: 38.5 us; the launch traced here: 38.4 us
  Pallas kernels  37.3 us (97%)
  local copies, waits for them, and re-layouts  1.02 us (3%)
    pallas_call x1, Pallas kernels, fused_body(): pl.pallas_call(functools.partial(kernel, near_spans, far_spans), out_shap...  37.3 us
    unnamed x1, local copies, waits for them, and re-layouts  1.02 us

profile of v1, /device:TPU:0, one launch (start us, length us, event | category | flops | bytes accessed | tf_op | source)
XLA Modules:
  0.0 38.4 jit_solution(7754096423995218883)
XLA Ops:
  0.0 37.3 %shard_map.64 = bf16[128,4608]{1,0:T(8,128)(2,1)S(1)} custom-call(s32[4]{0:T(128)} %index_hbm.1, s32[4]{0:T(128)} %live_hbm.1, bf16[512,1152]{1,0:T(8,128)(2,1)} %tok_hbm.1, bf16[1152,2304]{1,0:T(8,128)(2,1)} %w_hbm.1, bf16[64,16,1152]{2,1,0:T(8,128)(2,1)} %down_hbm.1, bf16[32,16,4608]{2,1,0:T(8,128)(2,1)} %up_hbm.1), custom_call_target="tpu_custom_call" | custom-call | tf_op jit(solution)/shard_map/pallas_call | solution.py:523
  37.3 1.0 %copy.8 = bf16[128,4608]{1,0:T(8,128)(2,1)} copy(bf16[128,4608]{1,0:T(8,128)(2,1)S(1)} %shard_map.64) | data formatting | bytes 2359296

commit v2 on v1

--- a/solution.py
+++ b/solution.py
@@ -10,7 +10,9 @@
 F32 = jnp.float32
 BF16 = jnp.bfloat16
 STAGES = 4
-FAR_PARTS = 3
+CUTS = 2
+NEAR = (2, 4, 4, 3, 5)
+FAR = (6, 8, 4)
 MESH = pl.DeviceIdType.MESH
 
 
@@ -111,6 +113,7 @@
     c_in,
     load_sem,
     w_sem,
+    send_sem,
     a_sem,
     fa_sem,
     b_sem,
@@ -139,15 +142,16 @@
     cols = w.shape[1]
     held, ranks, _ = up.shape
     part_rows = block // STAGES
+    piece = part_rows // CUTS
     near = len(near_spans)
     far = len(far_spans)
 
-    def remote(src, dst, sems, n, device):
+    def remote(src, dst, sent, sem, device):
         return pltpu.make_async_remote_copy(
             src_ref=src,
             dst_ref=dst,
-            send_sem=sems.at[0],
-            recv_sem=sems.at[1 + n],
+            send_sem=send_sem.at[sent],
+            recv_sem=sem,
             device_id=device,
             device_id_type=MESH,
         )
@@ -177,7 +181,6 @@
     w_loads += [w_load(n) for n in range(1, 3)]
     down_load = load(down_hbm, down, load_sem.at[4])
     w_loads += [w_load(n) for n in range(3, near)]
-    up_load = load(up_hbm, up, load_sem.at[5])
 
     barrier = pltpu.get_barrier_semaphore()
     for device in (x_peer, core_peer, y_peer, diagonal, z_peer):
@@ -188,14 +191,22 @@
         return copy
 
     x_copies, z_copies = [], []
-    for r in range(STAGES):
-        for y_at in (y_far, yy):
-            n = len(x_copies)
-            span = rows_at(2 * y_at + zp, r * part_rows, part_rows)
-            x_copies.append(remote(tok.at[span, :], far_tok.at[span, :], x_sem, n, x_peer))
-            z_copies.append(
-                remote(far_tok.at[span, :], far_tok.at[span, :], z_sem, n, z_peer)
-            )
+    for h in range(STAGES):
+        for r in range(CUTS):
+            for y_at in (y_far, yy):
+                span = rows_at(2 * y_at + zp, h * part_rows + r * piece, piece)
+                x_copies.append(
+                    remote(
+                        tok.at[span, :],
+                        far_tok.at[span, :],
+                        2,
+                        x_sem.at[len(x_copies)],
+                        x_peer,
+                    )
+                )
+                z_copies.append(
+                    remote(far_tok.at[span, :], far_tok.at[span, :], 2, z_sem.at[h], z_peer)
+                )
 
     def relay(n):
         x_copies[n].wait_recv()
@@ -223,7 +234,11 @@
         span = pl.ds(start, width)
         a_copies[u, n] = go(
             remote(
-                a_send.at[u, :, span], a_in.at[u, :, span], a_sem, u * near + n, core_peer
+                a_send.at[u, :, span],
+                a_in.at[u, :, span],
+                0,
+                a_sem.at[near if u else n],
+                core_peer,
             )
         )
 
@@ -232,7 +247,7 @@
         span = pl.ds(start, width)
         a_copies[0, n].wait_recv()
         b_send[:, span] = (keep[0, :, span] + a_in[0, :, span]).astype(BF16)
-        b_copies[n] = remote(b_send.at[:, span], b_in.at[:, span], b_sem, n, y_peer)
+        b_copies[n] = remote(b_send.at[:, span], b_in.at[:, span], 1, b_sem.at[n], y_peer)
         if not hold:
             go(b_copies[n])
 
@@ -253,7 +268,11 @@
         span = pl.ds(start, width)
         fa_copies[h, n] = go(
             remote(
-                fa_send.at[h, :, span], fa_in.at[h, :, span], fa_sem, h * far + n, core_peer
+                fa_send.at[h, :, span],
+                fa_in.at[h, :, span],
+                0,
+                fa_sem.at[h % 2 * far + n],
+                core_peer,
             )
         )
 
@@ -266,7 +285,13 @@
             BF16
         )
         fb_copies[h, n] = go(
-            remote(fb_send.at[h, :, span], fb_in.at[h, :, span], fb_sem, h * far + n, y_peer)
+            remote(
+                fb_send.at[h, :, span],
+                fb_in.at[h, :, span],
+                1,
+                fb_sem.at[h * far + n],
+                y_peer,
+            )
         )
 
     def far_return(h, n):
@@ -279,7 +304,13 @@
         total += peer_extra[pl.ds(h * part_rows, part_rows), span]
         c_send[h, :, span] = total.astype(BF16)
         c_copies[h, n] = go(
-            remote(c_send.at[h, :, span], c_in.at[h, :, span], c_sem, h * far + n, x_peer)
+            remote(
+                c_send.at[h, :, span],
+                c_in.at[h, :, span],
+                1,
+                c_sem.at[h + n if h == STAGES - 1 else h],
+                x_peer,
+            )
         )
 
     def expanded(low, factor):
@@ -297,7 +328,6 @@
     def finish_near(n):
         start, width = near_spans[n]
         span = pl.ds(start, width)
-        a_copies[1, n].wait_recv()
         b_copies[n].wait_recv()
         total = keep[1, :, span] + a_in[1, :, span] + b_in[:, span].astype(F32)
         factor = up_own[:, out_span(gx, start, width)] + up_in[:, span]
@@ -309,7 +339,10 @@
     def finish_far(h, n):
         start, width = far_spans[n]
         span = pl.ds(start, width)
-        c_copies[h, n].wait_recv()
+        if h == STAGES - 1:
+            c_copies[h, n].wait_recv()
+        elif n == 0:
+            remote(c_send.at[h], c_in.at[h], 1, c_sem.at[h], x_peer).wait_recv()
         rows = pl.ds(h * part_rows, part_rows)
         total = c_in[h, :, span].astype(F32) + far_extra[rows, span]
         out_ref[rows, out_span(1 - gx, start, width)] = jnp.where(
@@ -326,15 +359,17 @@
     w_loads[0].wait()
     near_dot(0, 0)
     tok_own_load.wait()
+    pl.semaphore_wait(barrier, 5)
+    early = len(x_copies) // 2
+    for n in range(2):
+        go(x_copies[n])
     index_load.wait()
     live_load.wait()
     name_send[...] = jnp.full(name_send.shape, index_ref[gy].astype(F32))
-    pl.semaphore_wait(barrier, 5)
+    name_copy = go(remote(name_send, name_in, 3, name_sem, x_peer))
+    for n in range(2, early):
+        go(x_copies[n])
     near_give(0, 0)
-    name_copy = go(remote(name_send, name_in, name_sem, 0, x_peer))
-    early = len(x_copies) - 2
-    for n in range(early):
-        go(x_copies[n])
 
     shrink_copies = []
 
@@ -349,10 +384,11 @@
     def shrink_give(d, device):
         shrink_send[d] = shrink_part(device["gy"])
         shrink_copies.append(
-            go(remote(shrink_send.at[d], shrink_in.at[d], shrink_sem, d, device))
+            go(remote(shrink_send.at[d], shrink_in.at[d], 3, shrink_sem, device))
         )
 
     near_step(0, 1)
+    up_load = load(up_hbm, up, load_sem.at[5])
     near_step(0, 2)
     near_pair(0)
     down_load.wait()
@@ -362,13 +398,11 @@
     near_step(0, 3)
     shrink_give(2, core_peer)
     near_pair(2)
-    for n in range(4, near):
-        near_step(0, n)
+    near_step(0, 4)
+    relay(0)
     shrink_own[...] = shrink_part(gy)
-    for n in range(3, near - 1):
-        near_pair(n)
-    relay(0)
-    near_pair(near - 1, hold=True)
+    near_pair(3)
+    relay(1)
 
     up_load.wait()
     slot = index_ref[gy] - gx * held
@@ -386,115 +420,142 @@
         factors = up[:, :, out_span(side, start, width)].reshape(held * ranks, width)
         return jnp.dot(pick, factors, preferred_element_type=F32).astype(BF16)
 
-    for start, width in far_spans:
-        up_send[:, pl.ds(start, width)] = picked(1 - gx, start, width)
-    for copy in shrink_copies:
-        copy.wait_recv()
+    def far_tokens(h):
+        half = pl.ds(0, 2 * part_rows)
+        remote(tok.at[half, :], far_tok.at[half, :], 2, z_sem.at[h], z_peer).wait_recv()
+
+    def pick_part(dst, side, n):
+        start, width = far_spans[n]
+        dst[:, pl.ds(start, width)] = picked(side, start, width)
+
+    pick_part(up_send, 1 - gx, 0)
+    pick_part(up_send, 1 - gx, 1)
+    relay(2)
+    pick_part(up_send, 1 - gx, 2)
+    remote(shrink_send, shrink_in, 3, shrink_sem, x_peer).wait_recv()
     shrink = (shrink_own[...] + shrink_in[0]) + (shrink_in[1] + shrink_in[2])
     low_send[...] = shrink.astype(BF16)
-    low_copy = go(remote(low_send, low_in, low_sem, 0, x_peer))
+    low_copy = go(remote(low_send, low_in, 3, low_sem, x_peer))
     for n in range(early, len(x_copies)):
         go(x_copies[n])
-    up_copy = go(remote(up_send, up_in, up_sem, 0, x_peer))
+    up_copy = go(remote(up_send, up_in, 1, up_sem, x_peer))
+    relay(3)
+    near_pair(4, hold=True)
+    pick_part(up_peer, gx, 0)
+    pick_part(up_peer, gx, 1)
+    relay(4)
+    pick_part(up_peer, gx, 2)
     near_step(1, 0)
+    relay(5)
     near_step(1, 1)
-    relay(1)
-    for start, width in far_spans:
-        up_peer[:, pl.ds(start, width)] = picked(gx, start, width)
+    relay(6)
     near_step(1, 2)
-    relay(2)
-    for n in range(3, near):
-        near_step(1, n)
-
-    relay(3)
-
-    def far_tokens(h):
-        z_copies[2 * h].wait_recv()
-        z_copies[2 * h + 1].wait_recv()
-
-    far_tokens(0)
-    for n in range(far):
-        far_dot(0, n)
-    relay(4)
-    for start, width in far_spans:
+    relay(7)
+
+    def peer_part(n):
+        start, width = far_spans[n]
+        span = pl.ds(start, width)
+        peer_extra[:, span] = expanded(low_in[...], up_peer[:, span])
+
+    def local_part(n):
+        start, width = far_spans[n]
         far_extra[:, pl.ds(start, width)] = expanded(
             low_send[...], up_own[:, out_span(1 - gx, start, width)]
         )
-    for n in range(far):
-        far_pair(0, n)
-    relay(5)
+
+    far_tokens(0)
+    far_dot(0, 0)
+    relay(8)
+    far_dot(0, 1)
+    relay(9)
+    far_dot(0, 2)
+    far_pair(0, 0)
+    low_copy.wait_recv()
+    peer_part(0)
+    far_pair(0, 1)
+    relay(10)
+    peer_part(1)
+    far_pair(0, 2)
+    peer_part(2)
+    relay(11)
+
     far_tokens(1)
-    for n in range(far):
-        far_dot(1, n)
-    relay(6)
-    low_copy.wait_recv()
-    for start, width in far_spans:
-        span = pl.ds(start, width)
-        peer_extra[:, span] = expanded(low_in[...], up_peer[:, span])
-    for n in range(far):
-        far_pair(1, n)
-    relay(7)
+    far_dot(1, 0)
+    relay(12)
+    far_dot(1, 1)
+    relay(13)
+    far_dot(1, 2)
+    far_pair(1, 0)
+    relay(14)
+    far_return(0, 0)
+    far_pair(1, 1)
+    relay(15)
+    far_pair(1, 2)
+    far_return(0, 1)
+
     far_tokens(2)
     far_dot(2, 0)
-    far_return(0, 0)
     far_dot(2, 1)
+    far_return(0, 2)
     far_dot(2, 2)
-    far_return(0, 1)
     far_pair(2, 0)
+    far_return(1, 0)
     far_pair(2, 1)
-    far_return(0, 2)
     far_pair(2, 2)
+
     far_tokens(3)
     far_dot(3, 0)
-    far_return(1, 0)
+    far_return(1, 1)
     far_dot(3, 1)
     far_dot(3, 2)
-    far_return(1, 1)
-    for n in range(far):
-        far_pair(3, n)
+    far_return(1, 2)
+    far_pair(3, 0)
+    far_pair(3, 1)
+    far_return(2, 0)
+    far_pair(3, 2)
     go(b_copies[near - 1])
-    far_return(1, 2)
-    up_copy.wait_recv()
-    for n in range(0, near - 1):
-        finish_near(n)
-    for n in range(far):
-        far_return(2, n)
+
+    near_step(1, 3)
+    far_return(2, 1)
+    near_step(1, 4)
+    local_part(0)
+    far_return(2, 2)
+    local_part(1)
+    local_part(2)
     for n in range(far):
         finish_far(0, n)
-    for n in range(far):
-        finish_far(1, n)
-    for n in range(far):
-        far_return(3, n)
-    for n in range(far):
-        finish_far(2, n)
+    up_copy.wait_recv()
+    far_return(3, 0)
+    remote(a_send.at[1], a_in.at[1], 0, a_sem.at[near], core_peer).wait_recv()
+    finish_near(0)
+    finish_near(1)
+    far_return(3, 1)
+    finish_near(2)
+    finish_near(3)
+    far_return(3, 2)
+    for h in range(1, STAGES - 1):
+        for n in range(far):
+            finish_far(h, n)
     finish_near(near - 1)
     for n in range(far):
-        finish_far(3, n)
-
-    half = pl.ds(0, 2 * block)
-    for src, sems in (
-        (a_send, a_sem),
-        (fa_send, fa_sem),
-        (b_send, b_sem),
-        (fb_send, fb_sem),
-        (c_send, c_sem),
-        (tok.at[half, :], x_sem),
-        (tok.at[half, :], z_sem),
-        (shrink_send, shrink_sem),
-        (name_send, name_sem),
-        (low_send, low_sem),
-        (up_send, up_sem),
-    ):
-        remote(src, src, sems, 0, x_peer).wait_send()
-
-
-def spans_of(cols, first, wide):
-    spans, start = [], 0
-    while start < cols:
-        width = min(wide if start else first, cols - start)
-        spans.append((start, width))
-        start += width
-    return spans
+        finish_far(STAGES - 1, n)
+
+    d2d = w.at[pl.ds(0, 8 * block), :]
+    remote(d2d, d2d, 0, name_sem, x_peer).wait_send()
+    links = w.at[pl.ds(0, 3 * block + ranks), :]
+    remote(links, links, 1, name_sem, x_peer).wait_send()
+    remote(tok, tok, 2, name_sem, x_peer).wait_send()
+    small = peer_extra.at[pl.ds(0, small_rows(ranks, block)), pl.ds(0, 128)]
+    remote(small, small, 3, name_sem, x_peer).wait_send()
+
+
+def small_rows(ranks, block):
+    return (14 * ranks * block + 8 * 128 * 4) // (128 * 4)
+
+
+def spans_of(cols, parts):
+    unit = cols // sum(parts)
+    return [(sum(parts[:n]) * unit, part * unit) for n, part in enumerate(parts)]
 
 
 def fused_body(
@@ -511,14 +572,13 @@
     block = rows // blocks
     count, ranks, _ = adapter_down_weight.shape
     held, _, out_width = adapter_up_weight.shape
-    near_spans = spans_of(cols, 256, 512)
-    far_spans = spans_of(cols, cols // FAR_PARTS, cols // FAR_PARTS)
+    near_spans = spans_of(cols, NEAR)
+    far_spans = spans_of(cols, FAR)
     near, far = len(near_spans), len(far_spans)
     part_rows = block // STAGES
     in_hbm = pl.BlockSpec(memory_space=pltpu.HBM)
 
-    def dma(n):
-        return pltpu.SemaphoreType.DMA((1 + n,))
+    dma = pltpu.SemaphoreType.DMA
 
     return pl.pallas_call(
         functools.partial(kernel, near_spans, far_spans),
@@ -558,19 +618,20 @@
             pltpu.VMEM((STAGES, part_rows, cols), BF16),
             pltpu.VMEM((STAGES, part_rows, cols), BF16),
             pltpu.VMEM((STAGES, part_rows, cols), BF16),
-            pltpu.SemaphoreType.DMA((6,)),
-            pltpu.SemaphoreType.DMA((near,)),
-            dma(2 * near),
-            dma(STAGES * far),
-            dma(near),
-            dma(STAGES * far),
-            dma(STAGES * far),
-            dma(2 * STAGES),
-            dma(2 * STAGES),
-            dma(3),
-            dma(1),
-            dma(1),
-            dma(1),
+            dma((6,)),
+            dma((near,)),
+            dma((4,)),
+            dma((near + 1,)),
+            dma((2 * far,)),
+            dma((near,)),
+            dma((STAGES * far,)),
+            dma((STAGES - 1 + far,)),
+            dma((2 * CUTS * STAGES,)),
+            dma((STAGES,)),
+            dma,
+            dma,
+            dma,
+            dma,
         ],
         compiler_params=pltpu.CompilerParams(
             collective_id=0, has_side_effects=True, vmem_limit_bytes=56 * 1024 * 1024
@@ -601,7 +662,7 @@
         blocks = arrays[4].shape[0]
         paired = sizes["gx"] == 2 and sizes["gy"] == 4 and sizes["gz"] % 2 == 0
         cols = arrays[1].shape[1]
-        cut = cols % (FAR_PARTS * 128) == 0 and len(spans_of(cols, 256, 512)) > 4
+        cut = cols % (sum(NEAR) * 128) == 0
         cut = cut and arrays[0].shape[0] // blocks % (STAGES * 16) == 0
         if paired and cut and blocks == sizes["gy"]:
             return fused_body(*arrays)

time: 38.5 us -> 36.1 us (0.938)
  Pallas kernels: 37.3 us -> 34.9 us
    pallas_call x1, Pallas kernels: 37.3 us -> 34.9 us  [fused_body(): pl.pallas_call(functools.partial(kernel, near_spans, far_spans), out_shap...]
where the time goes in v2:
time: 36.1 us; the launch traced here: 35.9 us
  Pallas kernels  34.9 us (97%)
  local copies, waits for them, and re-layouts  1.02 us (3%)
    pallas_call x1, Pallas kernels, fused_body(): pl.pallas_call(functools.partial(kernel, near_spans, far_spans), out_shap...  34.9 us
    unnamed x1, local copies, waits for them, and re-layouts  1.02 us

profile of v2, /device:TPU:0, one launch (start us, length us, event | category | flops | bytes accessed | tf_op | source)
XLA Modules:
  0.0 35.9 jit_solution(46066663455350620)
XLA Ops:
  0.0 34.9 %shard_map.64 = bf16[128,4608]{1,0:T(8,128)(2,1)S(1)} custom-call(s32[4]{0:T(128)} %index_hbm.1, s32[4]{0:T(128)} %live_hbm.1, bf16[512,1152]{1,0:T(8,128)(2,1)} %tok_hbm.1, bf16[1152,2304]{1,0:T(8,128)(2,1)} %w_hbm.1, bf16[64,16,1152]{2,1,0:T(8,128)(2,1)} %down_hbm.1, bf16[32,16,4608]{2,1,0:T(8,128)(2,1)} %up_hbm.1), custom_call_target="tpu_custom_call" | custom-call | tf_op jit(solution)/shard_map/pallas_call | solution.py:583
  34.9 1.0 %copy.8 = bf16[128,4608]{1,0:T(8,128)(2,1)} copy(bf16[128,4608]{1,0:T(8,128)(2,1)S(1)} %shard_map.64) | data formatting | bytes 2359296

commit v3 on v0

v3 whole, which is shorter than its diff:
```python
import functools

import jax
import jax.numpy as jnp
from jax import lax
from jax.experimental import pallas as pl
from jax.experimental.pallas import tpu as pltpu
from jax.sharding import PartitionSpec as P

F32 = jnp.float32
BF16 = jnp.bfloat16
STAGES = 4
CUTS = 2
NEAR = (2, 4, 4, 4, 4)
FAR = ((6, 8, 4),) * 4
PAIR = F32
MESH = pl.DeviceIdType.MESH


def general_body(
    tokens,
    base_up_weight,
    adapter_down_weight,
    adapter_up_weight,
    block_adapter_index,
    request_rows,
):
    rows, shard_width = tokens.shape
    groups = lax.axis_size("gy")
    blocks = block_adapter_index.shape[0]
    block = rows // blocks
    own_blocks = blocks // groups
    own_rows = own_blocks * block
    first = lax.axis_index("gy") * own_blocks
    count, rank_values, _ = adapter_down_weight.shape
    catalog = jnp.arange(count, dtype=jnp.int32)
    selected_adapters = (block_adapter_index[:, None] == catalog[None, :]).astype(BF16)
    chosen_down = jnp.dot(
        selected_adapters,
        adapter_down_weight.reshape(count, rank_values * shard_width),
        preferred_element_type=F32,
    )
    chosen_down = chosen_down.astype(BF16).reshape(blocks, rank_values, shard_width)
    tok_blocks = tokens.reshape(blocks, block, shard_width)
    shrink_part = jnp.einsum("bmd,brd->bmr", tok_blocks, chosen_down, preferred_element_type=F32)
    shrink_own = lax.psum_scatter(shrink_part, "gy", scatter_dimension=0, tiled=True)
    shrink_low = shrink_own.astype(BF16)
    adapter_factors = lax.all_gather(adapter_up_weight, "gx", axis=0, tiled=True)
    out_width = adapter_factors.shape[2]
    own_picks = lax.dynamic_slice_in_dim(selected_adapters, first, own_blocks, 0)
    chosen_up = jnp.dot(
        own_picks,
        adapter_factors.reshape(count, rank_values * out_width),
        preferred_element_type=F32,
    )
    chosen_up = chosen_up.astype(BF16).reshape(own_blocks, rank_values, out_width)
    expand = jnp.einsum("bmr,brf->bmf", shrink_low, chosen_up, preferred_element_type=F32)
    expand = expand.reshape(own_rows, out_width)
    partial_value = jnp.dot(
        tokens,
        lax.all_gather(base_up_weight, "gx", axis=1, tiled=True),
        preferred_element_type=F32,
    )
    extra = 2.0 * expand
    total = lax.psum_scatter(partial_value, "gy", scatter_dimension=0, tiled=True) + extra
    own_live = lax.dynamic_slice_in_dim(request_rows, first, own_blocks, 0)
    live_mask = (jnp.arange(block, dtype=jnp.int32)[None, :] < own_live[:, None]).reshape(
        own_rows, 1
    )
    return jnp.where(live_mask, total, 0.0).astype(BF16)


def kernel(
    near_spans,
    far_spans,
    index_hbm,
    live_hbm,
    tok_hbm,
    w_hbm,
    down_hbm,
    up_hbm,
    out_ref,
    index_ref,
    live_ref,
    tok,
    far_tok,
    w,
    down,
    up,
    name_send,
    name_in,
    up_own,
    up_send,
    up_in,
    up_peer,
    shrink_own,
    shrink_send,
    shrink_in,
    low_send,
    low_in,
    far_extra,
    peer_extra,
    a_send,
    a_in,
    keep,
    fa_send,
    fa_in,
    fkeep,
    b_send,
    b_in,
    fb_send,
    fb_in,
    c_send,
    c_in,
    send_sem,
    b_sem,
    c_sem,
    up_sem,
):
    gx = lax.axis_index("gx")
    gy = lax.axis_index("gy")
    gz = lax.axis_index("gz")
    core = lax.rem(gy, 2)
    yy = lax.div(gy, 2)
    y_far = 1 - yy
    zp = lax.rem(gz, 2)
    x_peer = {"gx": 1 - gx}
    core_peer = {"gy": gy + 1 - 2 * core}
    y_peer = {"gy": lax.rem(gy + 2, 4)}
    diagonal = {"gy": 3 - gy}
    z_peer = {"gz": gz + 1 - 2 * zp}
    block = out_ref.shape[0]
    cols = w.shape[1]
    held, ranks, _ = up.shape
    part_rows = block // STAGES
    piece = part_rows // CUTS
    near = len(near_spans)
    far = len(far_spans[0])

    def remote(src, dst, sent, sem, device):
        return pltpu.make_async_remote_copy(
            src_ref=src,
            dst_ref=dst,
            send_sem=send_sem.at[sent],
            recv_sem=sem,
            device_id=device,
            device_id_type=MESH,
        )

    def rows_at(block_at, first, count):
        return pl.ds(pl.multiple_of(block_at * block + first, count), count)

    def expanded(low, factor):
        return 2.0 * lax.dot_general(
            low, factor, (((0,), (0,)), ((), ())), preferred_element_type=F32
        )

    def live_rows(first, count):
        at = lax.broadcasted_iota(jnp.int32, (count, 1), 0) + first
        return at < live_ref[gy]

    def out_span(side, start, width):
        return pl.ds(pl.multiple_of(side * cols + start, 128), width)

    def finish_near(n):
        start, width = near_spans[n]
        span = pl.ds(start, width)
        remote(b_send.at[:, span], b_in.at[:, span], 1, b_sem.at[n], y_peer).wait_recv()
        total = keep[1, :, span] + b_in[:, span].astype(F32)
        out_ref[:, out_span(gx, start, width)] = jnp.where(
            live_rows(0, block), total, 0.0
        ).astype(BF16)

    def finish_far(h, n):
        start, width = far_spans[h][n]
        span = pl.ds(start, width)
        if h == STAGES - 1:
            remote(
                c_send.at[h, :, span],
                c_in.at[h, :, span],
                1,
                c_sem.at[h + n],
                x_peer,
            ).wait_recv()
        elif n == 0:
            remote(c_send.at[h], c_in.at[h], 1, c_sem.at[h], x_peer).wait_recv()
        rows = pl.ds(h * part_rows, part_rows)
        total = c_in[h, :, span].astype(F32) + far_extra[rows, span]
        out_ref[rows, out_span(1 - gx, start, width)] = jnp.where(
            live_rows(h * part_rows, part_rows), total, 0.0
        ).astype(BF16)

    def run(
        load_sem,
        w_sem,
        a_sem,
        fa_sem,
        fb_sem,
        x_sem,
        z_sem,
        shrink_sem,
        name_sem,
        low_sem,
    ):
        def load(src, dst, sem):
            copy = pltpu.make_async_copy(src, dst, sem)
            copy.start()
            return copy

        def tok_half(y_at, n):
            span = pl.ds(pl.multiple_of(y_at * 2 * block, 2 * block), 2 * block)
            return load(tok_hbm.at[span, :], tok.at[span, :], load_sem.at[n])

        def w_load(n):
            start, width = near_spans[n]
            span = pl.ds(start, width)
            return load(w_hbm.at[:, span], w.at[:, span], w_sem.at[n])

        tok_far_load = tok_half(y_far, 0)
        w_loads = [w_load(0)]
        tok_own_load = tok_half(yy, 1)
        index_load = load(index_hbm, index_ref, load_sem.at[2])
        live_load = load(live_hbm, live_ref, load_sem.at[3])
        w_loads += [w_load(n) for n in range(1, 3)]
        down_load = load(down_hbm, down, load_sem.at[4])
        w_loads += [w_load(n) for n in range(3, near)]

        barrier = pltpu.get_barrier_semaphore()
        for device in (x_peer, core_peer, y_peer, diagonal, z_peer):
            pl.semaphore_signal(barrier, inc=1, device_id=device, device_id_type=MESH)

        def go(copy):
            copy.start()
            return copy

        x_copies, z_copies = [], []
        for h in range(STAGES):
            for r in range(CUTS):
                for y_at in (y_far, yy):
                    span = rows_at(2 * y_at + zp, h * part_rows + r * piece, piece)
                    x_copies.append(
                        remote(
                            tok.at[span, :],
                            far_tok.at[span, :],
                            2,
                            x_sem.at[len(x_copies)],
                            x_peer,
                        )
                    )
                    z_copies.append(
                        remote(far_tok.at[span, :], far_tok.at[span, :], 2, z_sem.at[h], z_peer)
                    )

        def relay(n):
            x_copies[n].wait_recv()
            go(z_copies[n])

        a_copies, fa_copies, b_copies, fb_copies, c_copies = {}, {}, {}, {}, {}

        def near_dot(u, n):
            y_at = (y_far, yy)[u]
            start, width = near_spans[n]
            lhs = jnp.concatenate(
                [
                    tok[rows_at(2 * y_at + 1 - core, 0, block), :],
                    tok[rows_at(2 * y_at + core, 0, block), :],
                ],
                axis=0,
            )
            span = slice(start, start + width)
            part = jnp.dot(lhs, w[:, span], preferred_element_type=F32)
            a_send[u, :, span] = part[:block].astype(a_send.dtype)
            keep[u, :, span] = part[block:]

        def near_give(u, n):
            start, width = near_spans[n]
            span = pl.ds(start, width)
            a_copies[u, n] = go(
                remote(
                    a_send.at[u, :, span],
                    a_in.at[u, :, span],
                    0,
                    a_sem.at[near if u else n],
                    core_peer,
                )
            )

        def near_pair(n, hold=False):
            start, width = near_spans[n]
            span = pl.ds(start, width)
            a_copies[0, n].wait_recv()
            b_send[:, span] = (keep[0, :, span] + a_in[0, :, span].astype(F32)).astype(BF16)
            b_copies[n] = remote(b_send.at[:, span], b_in.at[:, span], 1, b_sem.at[n], y_peer)
            if not hold:
                go(b_copies[n])

        def far_dot(h, n):
            start, width = far_spans[h][n]
            lhs = jnp.concatenate(
                [
                    far_tok[rows_at(2 * y_at + c, h * part_rows, part_rows), :]
                    for c in (1 - core, core)
                    for y_at in (y_far, yy)
                ],
                axis=0,
            )
            span = slice(start, start + width)
            part = jnp.dot(lhs, w[:, span], preferred_element_type=F32)
            fa_send[h, :, span] = part[: 2 * part_rows].astype(fa_send.dtype)
            fkeep[h, :, span] = part[2 * part_rows :]
            span = pl.ds(start, width)
            fa_copies[h, n] = go(
                remote(
                    fa_send.at[h, :, span],
                    fa_in.at[h, :, span],
                    0,
                    fa_sem.at[h % 2 * far + n],
                    core_peer,
                )
            )

        def far_pair(h, n):
            start, width = far_spans[h][n]
            span = pl.ds(start, width)
            fa_copies[h, n].wait_recv()
            out_rows = pl.ds(0, part_rows)
            fb_send[h, :, span] = (
                fkeep[h, out_rows, span] + fa_in[h, out_rows, span].astype(F32)
            ).astype(BF16)
            fb_copies[h, n] = go(
                remote(
                    fb_send.at[h, :, span],
                    fb_in.at[h, :, span],
                    1,
                    fb_sem.at[h * far + n],
                    y_peer,
                )
            )

        def far_return(h, n):
            start, width = far_spans[h][n]
            span = pl.ds(start, width)
            own_rows = pl.ds(part_rows, part_rows)
            fb_copies[h, n].wait_recv()
            total = fkeep[h, own_rows, span] + fa_in[h, own_rows, span].astype(F32)
            total += fb_in[h, :, span].astype(F32)
            total += peer_extra[pl.ds(h * part_rows, part_rows), span]
            c_send[h, :, span] = total.astype(BF16)
            c_copies[h, n] = go(
                remote(
                    c_send.at[h, :, span],
                    c_in.at[h, :, span],
                    1,
                    c_sem.at[h + n if h == STAGES - 1 else h],
                    x_peer,
                )
            )

        def ready_near(n):
            start, width = near_spans[n]
            span = pl.ds(start, width)
            factor = up_own[:, out_span(gx, start, width)] + up_in[:, span]
            keep[1, :, span] += a_in[1, :, span].astype(F32) + expanded(low_send[...], factor)

        def near_step(u, n):
            if u == 0:
                w_loads[n].wait()
            near_dot(u, n)
            near_give(u, n)

        tok_far_load.wait()
        w_loads[0].wait()
        near_dot(0, 0)
        tok_own_load.wait()
        pl.semaphore_wait(barrier, 5)
        early = len(x_copies) // 2
        for n in range(2):
            go(x_copies[n])
        index_load.wait()
        live_load.wait()
        name_send[...] = jnp.full(name_send.shape, index_ref[gy].astype(F32))
        name_copy = go(remote(name_send, name_in, 3, name_sem, x_peer))
        for n in range(2, early):
            go(x_copies[n])
        near_give(0, 0)

        shrink_copies = []

        def shrink_part(at):
            return lax.dot_general(
                down[index_ref[at]],
                tok[rows_at(at, 0, block), :],
                (((1,), (1,)), ((), ())),
                preferred_element_type=F32,
            )

        def shrink_give(d, device):
            shrink_send[d] = shrink_part(device["gy"])
            shrink_copies.append(
                go(remote(shrink_send.at[d], shrink_in.at[d], 3, shrink_sem, device))
            )

        near_step(0, 1)
        up_load = load(up_hbm, up, load_sem.at[5])
        near_step(0, 2)
        near_pair(0)
        down_load.wait()
        shrink_give(0, y_peer)
        shrink_give(1, diagonal)
        near_pair(1)
        near_step(0, 3)
        shrink_give(2, core_peer)
        near_pair(2)
        near_step(0, 4)
        relay(0)
        shrink_own[...] = shrink_part(gy)
        near_pair(3)
        relay(1)

        up_load.wait()
        slot = index_ref[gy] - gx * held
        mine = up[jnp.clip(slot, 0, held - 1)]
        here = jnp.logical_and(slot >= 0, slot < held)
        up_own[...] = jnp.where(here, mine, jnp.zeros_like(mine))
        name_copy.wait_recv()
        rank_at = lax.broadcasted_iota(jnp.int32, (ranks, held * ranks), 0)
        slot_at = lax.broadcasted_iota(jnp.int32, (ranks, held * ranks), 1) + gx * held * ranks
        wanted = name_in[0:1, 0:1] * float(ranks)
        hit = (slot_at - rank_at).astype(F32) == wanted
        pick = jnp.where(hit, 1.0, 0.0).astype(BF16)

        def picked(side, start, width):
            factors = up[:, :, out_span(side, start, width)].reshape(held * ranks, width)
            return jnp.dot(pick, factors, preferred_element_type=F32).astype(BF16)

        def far_tokens(h):
            half = pl.ds(0, 2 * part_rows)
            remote(tok.at[half, :], far_tok.at[half, :], 2, z_sem.at[h], z_peer).wait_recv()

        def pick_part(dst, side, n):
            start, width = far_spans[1][n]
            dst[:, pl.ds(start, width)] = picked(side, start, width)

        pick_part(up_send, 1 - gx, 0)
        pick_part(up_send, 1 - gx, 1)
        relay(2)
        pick_part(up_send, 1 - gx, 2)
        remote(shrink_send, shrink_in, 3, shrink_sem, x_peer).wait_recv()
        shrink = (shrink_own[...] + shrink_in[0]) + (shrink_in[1] + shrink_in[2])
        low_send[...] = shrink.astype(BF16)
        low_copy = go(remote(low_send, low_in, 3, low_sem, x_peer))
        for n in range(early, len(x_copies)):
            go(x_copies[n])
        up_copy = go(remote(up_send, up_in, 1, up_sem, x_peer))
        relay(3)
        near_pair(4, hold=True)
        pick_part(up_peer, gx, 0)
        pick_part(up_peer, gx, 1)
        relay(4)
        pick_part(up_peer, gx, 2)
        near_step(1, 0)
        relay(5)
        near_step(1, 1)
        relay(6)
        near_step(1, 2)
        relay(7)

        def peer_part(n):
            start, width = far_spans[1][n]
            span = pl.ds(start, width)
            peer_extra[:, span] = expanded(low_in[...], up_peer[:, span])

        def local_part(n):
            start, width = far_spans[1][n]
            far_extra[:, pl.ds(start, width)] = expanded(
                low_send[...], up_own[:, out_span(1 - gx, start, width)]
            )

        far_tokens(0)
        far_dot(0, 0)
        relay(8)
        far_dot(0, 1)
        relay(9)
        far_dot(0, 2)
        far_pair(0, 0)
        low_copy.wait_recv()
        peer_part(0)
        far_pair(0, 1)
        relay(10)
        peer_part(1)
        far_pair(0, 2)
        peer_part(2)
        relay(11)

        far_tokens(1)
        far_dot(1, 0)
        relay(12)
        far_dot(1, 1)
        relay(13)
        far_dot(1, 2)
        far_pair(1, 0)
        relay(14)
        far_return(0, 0)
        far_pair(1, 1)
        relay(15)
        far_pair(1, 2)
        far_return(0, 1)

        far_tokens(2)
        far_dot(2, 0)
        far_dot(2, 1)
        far_return(0, 2)
        far_dot(2, 2)
        far_pair(2, 0)
        far_return(1, 0)
        far_pair(2, 1)
        far_pair(2, 2)

        far_tokens(3)
        far_dot(3, 0)
        far_return(1, 1)
        far_dot(3, 1)
        far_dot(3, 2)
        far_return(1, 2)
        far_pair(3, 0)
        far_pair(3, 1)
        far_return(2, 0)
        far_pair(3, 2)
        go(b_copies[near - 1])

        near_step(1, 3)
        far_return(2, 1)
        near_step(1, 4)
        local_part(0)
        far_return(2, 2)
        local_part(1)
        local_part(2)
        for n in range(far):
            finish_far(0, n)
        up_copy.wait_recv()
        far_return(3, 0)
        remote(a_send.at[1], a_in.at[1], 0, a_sem.at[near], core_peer).wait_recv()
        ready_near(0)
        ready_near(1)
        ready_near(2)
        far_return(3, 1)
        ready_near(3)
        far_return(3, 2)
        ready_near(4)

    dma = pltpu.SemaphoreType.DMA
    pl.run_scoped(
        run,
        dma((6,)),
        dma((near,)),
        dma((near + 1,)),
        dma((2 * far,)),
        dma((STAGES * far,)),
        dma((2 * CUTS * STAGES,)),
        dma((STAGES,)),
        dma,
        dma,
        dma,
    )
    for n in range(near - 1):
        finish_near(n)
    for h in range(1, STAGES - 1):
        for n in range(far):
            finish_far(h, n)
    for n in range(far - 1):
        finish_far(STAGES - 1, n)
    finish_near(near - 1)
    finish_far(STAGES - 1, far - 1)

    d2d = w.at[pl.ds(0, 2 * jnp.dtype(PAIR).itemsize * block), :]
    remote(d2d, d2d, 0, up_sem, x_peer).wait_send()
    links = w.at[pl.ds(0, 3 * block + ranks), :]
    remote(links, links, 1, up_sem, x_peer).wait_send()
    remote(tok, tok, 2, up_sem, x_peer).wait_send()
    small = peer_extra.at[pl.ds(0, small_rows(ranks, block)), pl.ds(0, 128)]
    remote(small, small, 3, up_sem, x_peer).wait_send()


def small_rows(ranks, block):
    return (14 * ranks * block + 8 * 128 * 4) // (128 * 4)


def spans_of(cols, parts):
    unit = cols // sum(parts)
    return [(sum(parts[:n]) * unit, part * unit) for n, part in enumerate(parts)]


def fused_body(
    tokens,
    base_up_weight,
    adapter_down_weight,
    adapter_up_weight,
    block_adapter_index,
    request_rows,
):
    rows, depth = tokens.shape
    cols = base_up_weight.shape[1]
    blocks = block_adapter_index.shape[0]
    block = rows // blocks
    count, ranks, _ = adapter_down_weight.shape
    held, _, out_width = adapter_up_weight.shape
    near_spans = spans_of(cols, NEAR)
    far_spans = [spans_of(cols, parts) for parts in FAR]
    near, far = len(near_spans), len(far_spans[0])
    part_rows = block // STAGES
    in_hbm = pl.BlockSpec(memory_space=pltpu.HBM)

    dma = pltpu.SemaphoreType.DMA

    return pl.pallas_call(
        functools.partial(kernel, near_spans, far_spans),
        out_shape=pltpu.VMEM((block, out_width), BF16),
        in_specs=[in_hbm] * 6,
        out_specs=pl.BlockSpec(memory_space=pltpu.VMEM),
        scratch_shapes=[
            pltpu.SMEM((blocks,), jnp.int32),
            pltpu.SMEM((blocks,), jnp.int32),
            pltpu.VMEM((rows, depth), BF16),
            pltpu.VMEM((rows, depth), BF16),
            pltpu.VMEM((depth, cols), BF16),
            pltpu.VMEM((count, ranks, depth), BF16),
            pltpu.VMEM((held, ranks, out_width), BF16),
            pltpu.VMEM((8, 128), F32),
            pltpu.VMEM((8, 128), F32),
            pltpu.VMEM((ranks, out_width), BF16),
            pltpu.VMEM((ranks, cols), BF16),
            pltpu.VMEM((ranks, cols), BF16),
            pltpu.VMEM((ranks, cols), BF16),
            pltpu.VMEM((ranks, block), F32),
            pltpu.VMEM((3, ranks, block), F32),
            pltpu.VMEM((3, ranks, block), F32),
            pltpu.VMEM((ranks, block), BF16),
            pltpu.VMEM((ranks, block), BF16),
            pltpu.VMEM((block, cols), F32),
            pltpu.VMEM((block, cols), F32),
            pltpu.VMEM((2, block, cols), PAIR),
            pltpu.VMEM((2, block, cols), PAIR),
            pltpu.VMEM((2, block, cols), F32),
            pltpu.VMEM((STAGES, 2 * part_rows, cols), PAIR),
            pltpu.VMEM((STAGES, 2 * part_rows, cols), PAIR),
            pltpu.VMEM((STAGES, 2 * part_rows, cols), F32),
            pltpu.VMEM((block, cols), BF16),
            pltpu.VMEM((block, cols), BF16),
            pltpu.VMEM((STAGES, part_rows, cols), BF16),
            pltpu.VMEM((STAGES, part_rows, cols), BF16),
            pltpu.VMEM((STAGES, part_rows, cols), BF16),
            pltpu.VMEM((STAGES, part_rows, cols), BF16),
            dma((4,)),
            dma((near,)),
            dma((STAGES - 1 + far,)),
            dma,
        ],
        compiler_params=pltpu.CompilerParams(
            collective_id=0, has_side_effects=True, vmem_limit_bytes=56 * 1024 * 1024
        ),
    )(
        block_adapter_index,
        request_rows,
        tokens,
        base_up_weight,
        adapter_down_weight,
        adapter_up_weight,
    )


def solution(mesh):
    in_specs = (
        P("gx", "gy"),
        P("gy", ("gz", "gx")),
        P(None, None, "gy"),
        P("gx", None, "gz"),
        P("gx"),
        P("gx"),
    )
    out_specs = P(("gx", "gy"), "gz")
    sizes = mesh.shape

    def body(*arrays):
        blocks = arrays[4].shape[0]
        paired = sizes["gx"] == 2 and sizes["gy"] == 4 and sizes["gz"] % 2 == 0
        cols = arrays[1].shape[1]
        cut = cols % (sum(NEAR) * 128) == 0
        cut = cut and arrays[0].shape[0] // blocks % (STAGES * 16) == 0
        if paired and cut and blocks == sizes["gy"]:
            return fused_body(*arrays)
        return general_body(*arrays)

    return jax.shard_map(body, mesh=mesh, in_specs=in_specs, out_specs=out_specs, check_vma=False)
```

time: 50.8 us -> 35.2 us (0.69)
  Pallas kernels: 48.3 us -> 34 us
  local copies, waits for them, and re-layouts: 2.36 us -> 1.02 us
    pallas_call x1, Pallas kernels: 48.3 us -> 34 us  [fused_body(): pl.pallas_call(functools.partial(kernel, near_spans, far_spans), out_shap...]
    unnamed x1, local copies, waits for them, and re-layouts: 2.36 us -> 1.02 us
where the time goes in v3:
time: 35.2 us; the launch traced here: 35.1 us
  Pallas kernels  34 us (97%)
  local copies, waits for them, and re-layouts  1.02 us (3%)
    pallas_call x1, Pallas kernels, fused_body(): pl.pallas_call(functools.partial(kernel, near_spans, far_spans), out_shap...  34 us
    unnamed x1, local copies, waits for them, and re-layouts  1.02 us

profile of v3, /device:TPU:0, one launch (start us, length us, event | category | flops | bytes accessed | tf_op | source)
XLA Modules:
  0.0 35.1 jit_solution(11244031434335048620)
XLA Ops:
  0.0 34.0 %shard_map.64 = bf16[128,4608]{1,0:T(8,128)(2,1)S(1)} custom-call(s32[4]{0:T(128)} %index_hbm.1, s32[4]{0:T(128)} %live_hbm.1, bf16[512,1152]{1,0:T(8,128)(2,1)} %tok_hbm.1, bf16[1152,2304]{1,0:T(8,128)(2,1)} %w_hbm.1, bf16[64,16,1152]{2,1,0:T(8,128)(2,1)} %down_hbm.1, bf16[32,16,4608]{2,1,0:T(8,128)(2,1)} %up_hbm.1), custom_call_target="tpu_custom_call" | custom-call | tf_op jit(solution)/shard_map/pallas_call | solution.py:615
  34.0 1.0 %copy.8 = bf16[128,4608]{1,0:T(8,128)(2,1)} copy(bf16[128,4608]{1,0:T(8,128)(2,1)S(1)} %shard_map.64) | data formatting | bytes 2359296

commit v4 on v3

--- a/solution.py
+++ b/solution.py
@@ -113,9 +113,8 @@
     c_send,
     c_in,
     send_sem,
-    b_sem,
-    c_sem,
-    up_sem,
+    b_last,
+    c_last,
 ):
     gx = lax.axis_index("gx")
     gy = lax.axis_index("gy")
@@ -162,16 +161,16 @@
     def out_span(side, start, width):
         return pl.ds(pl.multiple_of(side * cols + start, 128), width)
 
-    def finish_near(n):
+    def finish_near(n, sem):
         start, width = near_spans[n]
         span = pl.ds(start, width)
-        remote(b_send.at[:, span], b_in.at[:, span], 1, b_sem.at[n], y_peer).wait_recv()
+        remote(b_send.at[:, span], b_in.at[:, span], 1, sem, y_peer).wait_recv()
         total = keep[1, :, span] + b_in[:, span].astype(F32)
         out_ref[:, out_span(gx, start, width)] = jnp.where(
             live_rows(0, block), total, 0.0
         ).astype(BF16)
 
-    def finish_far(h, n):
+    def finish_far(h, n, sem):
         start, width = far_spans[h][n]
         span = pl.ds(start, width)
         if h == STAGES - 1:
@@ -179,11 +178,11 @@
                 c_send.at[h, :, span],
                 c_in.at[h, :, span],
                 1,
-                c_sem.at[h + n],
+                sem,
                 x_peer,
             ).wait_recv()
         elif n == 0:
-            remote(c_send.at[h], c_in.at[h], 1, c_sem.at[h], x_peer).wait_recv()
+            remote(c_send.at[h], c_in.at[h], 1, sem, x_peer).wait_recv()
         rows = pl.ds(h * part_rows, part_rows)
         total = c_in[h, :, span].astype(F32) + far_extra[rows, span]
         out_ref[rows, out_span(1 - gx, start, width)] = jnp.where(
@@ -201,6 +200,9 @@
         shrink_sem,
         name_sem,
         low_sem,
+        b_sem,
+        c_sem,
+        up_sem,
     ):
         def load(src, dst, sem):
             copy = pltpu.make_async_copy(src, dst, sem)
@@ -290,7 +292,7 @@
             span = pl.ds(start, width)
             a_copies[0, n].wait_recv()
             b_send[:, span] = (keep[0, :, span] + a_in[0, :, span].astype(F32)).astype(BF16)
-            b_copies[n] = remote(b_send.at[:, span], b_in.at[:, span], 1, b_sem.at[n], y_peer)
+            b_copies[n] = remote(b_send.at[:, span], b_in.at[:, span], 1, b_last if n == near - 1 else b_sem.at[n], y_peer)
             if not hold:
                 go(b_copies[n])
 
@@ -351,7 +353,7 @@
                     c_send.at[h, :, span],
                     c_in.at[h, :, span],
                     1,
-                    c_sem.at[h + n if h == STAGES - 1 else h],
+                    c_last.at[n] if h == STAGES - 1 else c_sem.at[h],
                     x_peer,
                 )
             )
@@ -536,7 +538,7 @@
         local_part(1)
         local_part(2)
         for n in range(far):
-            finish_far(0, n)
+            finish_far(0, n, c_sem.at[0])
         up_copy.wait_recv()
         far_return(3, 0)
         remote(a_send.at[1], a_in.at[1], 0, a_sem.at[near], core_peer).wait_recv()
@@ -547,6 +549,11 @@
         ready_near(3)
         far_return(3, 2)
         ready_near(4)
+        for n in range(near - 1):
+            finish_near(n, b_sem.at[n])
+        for h in range(1, STAGES - 1):
+            for n in range(far):
+                finish_far(h, n, c_sem.at[h])
 
     dma = pltpu.SemaphoreType.DMA
     pl.run_scoped(
@@ -561,24 +568,22 @@
         dma,
         dma,
         dma,
+        dma((near - 1,)),
+        dma((STAGES - 1,)),
+        dma,
     )
-    for n in range(near - 1):
-        finish_near(n)
-    for h in range(1, STAGES - 1):
-        for n in range(far):
-            finish_far(h, n)
     for n in range(far - 1):
-        finish_far(STAGES - 1, n)
-    finish_near(near - 1)
-    finish_far(STAGES - 1, far - 1)
+        finish_far(STAGES - 1, n, c_last.at[n])
+    finish_near(near - 1, b_last)
+    finish_far(STAGES - 1, far - 1, c_last.at[far - 1])
 
     d2d = w.at[pl.ds(0, 2 * jnp.dtype(PAIR).itemsize * block), :]
-    remote(d2d, d2d, 0, up_sem, x_peer).wait_send()
+    remote(d2d, d2d, 0, b_last, x_peer).wait_send()
     links = w.at[pl.ds(0, 3 * block + ranks), :]
-    remote(links, links, 1, up_sem, x_peer).wait_send()
-    remote(tok, tok, 2, up_sem, x_peer).wait_send()
+    remote(links, links, 1, b_last, x_peer).wait_send()
+    remote(tok, tok, 2, b_last, x_peer).wait_send()
     small = peer_extra.at[pl.ds(0, small_rows(ranks, block)), pl.ds(0, 128)]
-    remote(small, small, 3, up_sem, x_peer).wait_send()
+    remote(small, small, 3, b_last, x_peer).wait_send()
 
 
 def small_rows(ranks, block):
@@ -651,9 +656,8 @@
             pltpu.VMEM((STAGES, part_rows, cols), BF16),
             pltpu.VMEM((STAGES, part_rows, cols), BF16),
             dma((4,)),
-            dma((near,)),
-            dma((STAGES - 1 + far,)),
             dma,
+            dma((far,)),
         ],
         compiler_params=pltpu.CompilerParams(
             collective_id=0, has_side_effects=True, vmem_limit_bytes=56 * 1024 * 1024

time: 35.2 us -> 35.1 us (level)
  no operation moved by 1% of the time
where the time goes in v4:
time: 35.1 us; the launch traced here: 35 us
  Pallas kernels  34 us (97%)
  local copies, waits for them, and re-layouts  1.02 us (3%)
    pallas_call x1, Pallas kernels, fused_body(): pl.pallas_call(functools.partial(kernel, near_spans, far_spans), out_shap...  34 us
    unnamed x1, local copies, waits for them, and re-layouts  1.02 us

profile of v4, /device:TPU:0, one launch (start us, length us, event | category | flops | bytes accessed | tf_op | source)
XLA Modules:
  0.0 35.0 jit_solution(7692406203080218571)
XLA Ops:
  0.0 34.0 %shard_map.64 = bf16[128,4608]{1,0:T(8,128)(2,1)S(1)} custom-call(s32[4]{0:T(128)} %index_hbm.1, s32[4]{0:T(128)} %live_hbm.1, bf16[512,1152]{1,0:T(8,128)(2,1)} %tok_hbm.1, bf16[1152,2304]{1,0:T(8,128)(2,1)} %w_hbm.1, bf16[64,16,1152]{2,1,0:T(8,128)(2,1)} %down_hbm.1, bf16[32,16,4608]{2,1,0:T(8,128)(2,1)} %up_hbm.1), custom_call_target="tpu_custom_call" | custom-call | tf_op jit(solution)/shard_map/pallas_call | solution.py:620
  34.0 1.0 %copy.8 = bf16[128,4608]{1,0:T(8,128)(2,1)} copy(bf16[128,4608]{1,0:T(8,128)(2,1)S(1)} %shard_map.64) | data formatting | bytes 2359296
